TPU v7x, 32 devices: a whole 2x2x4 slice. The times are simulated.
32 devices in a mesh: cuts: 8 (over z, y), event: 4 (over x, core).
Axes of the slice: x: 2, y: 2, z: 4, core: 2. Of those that a mesh axis runs over, the one named last changes fastest.
Arguments:
- kernels: float32 [4, 64, 128, 256], P('event', 'cuts'), may hold values from -24 to 24
- steps: float32 [8, 64, 128, 256], P(None, 'cuts', 'event'), may hold values from -11 to 11
- curvature: float32 [8, 64, 128, 256], P(None, 'cuts', 'event'), may hold values from 0.2 to 5
Outputs:
- gradient: float32 [64, 128, 256], P('cuts', 'event')
- direction: float32 [64, 128, 256], P('cuts', 'event')
All inputs are finite; a program needn't handle non-finite values.
Results may differ from a plain program's by a relative error of at most 0.00021.
Values sent between devices are 32-bit elements; how exact they have to be, the bound alone decides.
A program may use at most 64 MiB of HBM per device.

v0:
```python
import functools
import math

import jax
import jax.numpy as jnp
from jax import lax
from jax.experimental import pallas as pl
from jax.experimental.pallas import tpu as pltpu
from jax.sharding import PartitionSpec as P

RIM = 4
SPLIT = 2
LANES = 128
SUB = 8
MESH = pl.DeviceIdType.MESH
HIGHEST = lax.Precision.HIGHEST


def cycle_weights():
    unscaled = [math.exp(-((column - RIM) ** 2) / 4.5) for column in range(2 * RIM + 1)]
    whole = sum(unscaled)
    return [weight / whole for weight in unscaled]


def halves(value):
    high = value.astype(jnp.bfloat16)
    return high, (value - high.astype(jnp.float32)).astype(jnp.bfloat16)


def unscaled_gauss(length, sigma):
    rows = lax.broadcasted_iota(jnp.int32, (length, length), 0)
    columns = lax.broadcasted_iota(jnp.int32, (length, length), 1)
    offset = (rows - columns).astype(jnp.float32)
    return jnp.exp(-offset * offset / (2.0 * sigma * sigma))


def upper(pairs):
    return [(i, j) for i in range(pairs) for j in range(i, pairs)]


def kernel(
    sizes,
    kern_hbm, steps_hbm, curv_hbm, grad, steps, changes, coef,
    kern, rad, far_in, near_in, far_out, x_in, plane, halo_in,
    rad_mat, lat_mat, gram_acc, gram_row, gram_all,
    table, splat, mix, late_row, late_all,
    load_sem, core_send, core_recv, x_send, x_recv, halo_send, halo_recv,
    gram_send, gram_recv, late_send, late_recv,
):
    n_c, n_e, pairs, rad_len, lat_len = sizes
    part = rad_len // n_e
    c = lax.axis_index("cuts")
    e = lax.axis_index("event")
    barrier = pltpu.get_barrier_semaphore()
    others = [
        {"cuts": lax.rem(c + d // n_e, n_c), "event": lax.rem(e + d % n_e, n_e)}
        for d in range(1, n_c * n_e)
    ]
    for other in others:
        pl.semaphore_signal(barrier, 1, device_id=other, device_id_type=MESH)

    loads = [
        pltpu.make_async_copy(kern_hbm.at[:, k], kern.at[:, k], load_sem.at[k]) for k in range(RIM)
    ]
    loads.append(pltpu.make_async_copy(steps_hbm, steps, load_sem.at[RIM]))
    loads.append(pltpu.make_async_copy(curv_hbm, changes, load_sem.at[RIM + 1]))
    for load in loads:
        load.start()

    matrix = unscaled_gauss(rad_len, 3.0)
    high, low = halves(matrix / jnp.sum(matrix, axis=1, keepdims=True))
    rad_mat[...] = jnp.concatenate([high, high, low], axis=1)
    matrix = unscaled_gauss(lat_len, 4.0)
    high, low = halves(matrix / jnp.sum(matrix, axis=0, keepdims=True))
    lat_mat[...] = jnp.concatenate([high, high, low], axis=0)
    table[...] = jnp.zeros_like(table)

    core = e + 1 - 2 * lax.rem(e, 2)
    far = lax.rem(e + 2, n_e)
    core_far = lax.rem(core + 2, n_e)

    def rows(chunk):
        return pl.ds(pl.multiple_of(chunk * part, part), part)

    def send(src, dst, send_sem, recv_sem, where):
        return pltpu.make_async_remote_copy(
            src_ref=src, dst_ref=dst, send_sem=send_sem, recv_sem=recv_sem,
            device_id=where, device_id_type=MESH,
        )

    far_copies, near_copies, x_copies, halo_copies = [], [], [], []
    for k in range(RIM):
        loads[k].wait()
        for side in range(2):
            high, low = halves(kern[side, k])
            rad[side, k] = jnp.dot(
                rad_mat[...], jnp.concatenate([high, low, high], axis=0),
                preferred_element_type=jnp.float32,
            )
    pl.semaphore_wait(barrier, len(others))
    for k in range(RIM):
        far_copies.append(send(
            rad.at[:, k, rows(core_far)], far_in.at[:, k], core_send.at[0, k], core_recv.at[0, k],
            {"event": core},
        ))
        far_copies[-1].start()
    for k in range(RIM):
        near_copies.append(send(
            rad.at[:, k, rows(core)], near_in.at[:, k], core_send.at[1, k], core_recv.at[1, k],
            {"event": core},
        ))
        near_copies[-1].start()
    strips = part // SUB
    step_k = RIM // SPLIT
    pieces = [(h, g) for h in range(strips) for g in range(SPLIT)]

    def strip_rows(chunk, h):
        return pl.ds(pl.multiple_of(chunk * part + h * SUB, SUB), SUB)

    for h, g in pieces:
        ks = pl.ds(g * step_k, step_k)
        if h == 0:
            for k in range(g * step_k, (g + 1) * step_k):
                far_copies[k].wait_recv()
        here = pl.ds(h * SUB, SUB)
        far_out[:, ks, here] = rad[:, ks, strip_rows(far, h)] + far_in[:, ks, here]
        x_copies.append(send(
            far_out.at[:, ks, here], x_in.at[:, ks, here], x_send.at[h, g], x_recv.at[h, g],
            {"event": far},
        ))
        x_copies[-1].start()

    slots = {pair: number for number, pair in enumerate(upper(pairs))}
    count = len(slots)
    groups = [(0, 1), (2, 3), tuple(range(4, pairs))]
    all_rows = steps.shape[1]
    tiles = all_rows // SUB
    lats = lat_len // LANES
    strip = tiles // RIM

    def gram(number):
        if number == 0:
            loads[RIM].wait()
            loads[RIM + 1].wait()

        def scale(t, _):
            place = pl.ds(pl.multiple_of(t * SUB, SUB), SUB)
            for i in range(pairs):
                changes[i, place, :] = changes[i, place, :] * steps[i, place, :]
            return 0

        lax.fori_loop(number * strip, (number + 1) * strip, scale, 0, unroll=2)
        for group in groups:
            wanted = [(i, j) for i in group for j in range(i, pairs)]

            def body(t, sums):
                place = pl.ds(pl.multiple_of(t * SUB, SUB), SUB)
                sums = list(sums)
                for lane in range(lats):
                    across = pl.ds(lane * LANES, LANES)
                    change = {j: changes[j, place, across] for j in range(group[0], pairs)}
                    for n, i in enumerate(group):
                        step = steps[i, place, across]
                        for m, (a, b) in enumerate(wanted):
                            if a == i:
                                sums[2 * m] = sums[2 * m] + step * change[b]
                                sums[2 * m + 1] = sums[2 * m + 1] + change[i] * change[b]
                return tuple(sums)

            sums = lax.fori_loop(
                number * strip, (number + 1) * strip, body,
                tuple(jnp.zeros((SUB, LANES), jnp.float32) for _ in range(2 * len(wanted))),
            )
            for m, pair in enumerate(wanted):
                for kind in range(2):
                    place = slots[pair] + kind * count
                    if number == 0:
                        gram_acc[place] = sums[2 * m + kind]
                    else:
                        gram_acc[place] = gram_acc[place] + sums[2 * m + kind]

    def spread(row, slot_refs, sends, recvs):
        copies = []
        for d, other in enumerate(others):
            copies.append(send(row, slot_refs.at[d], sends.at[d], recvs.at[d], other))
            copies[-1].start()
        return copies

    def gathered(row, slot_refs, copies):
        for copy in copies:
            copy.wait_recv()
        return row[...] + jnp.sum(slot_refs[...], axis=0)

    def arrive(h):
        here = pl.ds(h * SUB, SUB)
        for g in range(SPLIT):
            ks = pl.ds(g * step_k, step_k)
            if h == 0:
                for k in range(g * step_k, (g + 1) * step_k):
                    near_copies[k].wait_recv()
            base = rad[:, ks, strip_rows(e, h)] + near_in[:, ks, here]
            x_copies[h * SPLIT + g].wait_recv()
            whole = (base + x_in[:, ks, here]).reshape(2 * step_k * SUB, lat_len)
            high, low = halves(whole)
            plane[:, ks, here] = jnp.dot(
                jnp.concatenate([high, low, high], axis=1), lat_mat[...],
                preferred_element_type=jnp.float32,
            ).reshape(2, step_k, SUB, lat_len)
            odd = lax.rem(c, 2)
            for side in (odd, 1 - odd):
                halo_copies.append(send(
                    plane.at[side, ks, here], halo_in.at[side, ks, here],
                    halo_send.at[side, h, g], halo_recv.at[side, h, g],
                    {"cuts": lax.rem(c + n_c - 1 + 2 * side, n_c)},
                ))
                halo_copies[-1].start()

    weights = cycle_weights()
    lons = 2 * RIM

    def finish(h):
        for copy in halo_copies[2 * SPLIT * h : 2 * SPLIT * (h + 1)]:
            copy.wait_recv()
        sums = [None] * (2 * pairs)
        for lane in range(lats):
            place, across = pl.ds(h * SUB, SUB), pl.ds(lane * LANES, LANES)
            padded = (
                [halo_in[1, k, place, across] for k in range(RIM)]
                + [plane[side, k, place, across] for side in range(2) for k in range(RIM)]
                + [halo_in[0, k, place, across] for k in range(RIM)]
            )
            for a in range(lons):
                value = weights[RIM] * padded[a + RIM]
                for k in range(1, RIM + 1):
                    value = value + weights[RIM + k] * (padded[a + RIM - k] + padded[a + RIM + k])
                spot = pl.ds(a * part + h * SUB, SUB)
                grad[spot, across] = value
                for i in range(pairs):
                    for n, vector in ((i, steps), (pairs + i, changes)):
                        term = value * vector[i, spot, across]
                        sums[n] = term if sums[n] is None else sums[n] + term
        for n in range(2 * pairs):
            place = pl.ds(n * SUB, SUB)
            table[place, :] = sums[n] if h == 0 else table[place, :] + sums[n]

    gram(0)
    gram(1)
    arrive(0)
    gram(2)
    arrive(1)
    gram(3)
    ones = jnp.ones((LANES, LANES), jnp.float32)

    def lane_sums(value):
        return lax.dot_general(
            ones[:SUB], value, (((1,), (1,)), ((), ())), precision=HIGHEST,
            preferred_element_type=jnp.float32,
        )[:1]

    table[pl.ds(0, 2 * count), :] = jnp.sum(gram_acc[...], axis=1)
    gram_row[...] = lane_sums(table[...])
    gram_copies = spread(gram_row, gram_all, gram_send, gram_recv)
    for h in range(2, strips):
        arrive(h)
    for h in range(strips):
        finish(h)
    first, _ = halves(table[...])
    second, third = halves(table[...] - first.astype(jnp.float32))
    late_row[...] = lax.dot_general(
        jnp.ones((SUB, 3 * LANES), jnp.bfloat16), jnp.concatenate([first, second, third], axis=1),
        (((1,), (1,)), ((), ())), preferred_element_type=jnp.float32,
    )[:1]
    late_copies = spread(late_row, late_all, late_send, late_recv)
    products = gathered(gram_row, gram_all, gram_copies)
    square = (LANES, LANES)
    on_diagonal = lax.broadcasted_iota(jnp.int32, square, 0) == lax.broadcasted_iota(jnp.int32, square, 1)
    splat[...] = jnp.dot(
        jnp.where(on_diagonal, jnp.broadcast_to(products, square), 0.0), ones,
        precision=HIGHEST, preferred_element_type=jnp.float32,
    )

    def cross(i, j):
        place = slots[i, j]
        return splat[place : place + 1, :]

    def squared(i, j):
        place = count + slots[min(i, j), max(i, j)]
        return splat[place : place + 1, :]

    def unit(place):
        return (lax.broadcasted_iota(jnp.int32, (1, LANES), 1) // SUB == place).astype(jnp.float32)

    inverse = [1.0 / cross(i, i) for i in range(pairs)]
    scaling = cross(pairs - 1, pairs - 1) / squared(pairs - 1, pairs - 1)
    alphas = [None] * pairs
    for i in reversed(range(pairs)):
        row = unit(i)
        for j in range(pairs - 1, i, -1):
            row = row - cross(i, j) * alphas[j]
        alphas[i] = inverse[i] * row
    onto = []
    for i in range(pairs):
        row = unit(pairs + i)
        for j in range(pairs):
            row = row - squared(i, j) * alphas[j]
        row = scaling * row
        for j in range(i):
            row = row + cross(j, i) * onto[j]
        onto.append(alphas[i] - inverse[i] * row)
    for i in range(pairs):
        mix[i : i + 1, :] = -onto[i]
        mix[pairs + i : pairs + i + 1, :] = scaling * alphas[i]

    products = gathered(late_row, late_all, late_copies)
    mixed = jnp.sum(mix[...] * products, axis=1, keepdims=True)
    coef[pl.ds(0, 2 * pairs), :] = jnp.broadcast_to(mixed, (2 * pairs, LANES))
    coef[pl.ds(2 * pairs, SUB), :] = jnp.broadcast_to(-scaling, (SUB, LANES))
    for copies in (far_copies, near_copies, x_copies, halo_copies, gram_copies, late_copies):
        for copy in copies:
            copy.wait_send()


def combine_kernel(pairs, blocks, grad, steps, changes, coef, grad_hbm, dir_hbm, direc, sems):
    grad_out = pltpu.make_async_copy(grad, grad_hbm, sems.at[blocks])
    grad_out.start()
    all_rows, lat_len = grad.shape
    ratio = jnp.broadcast_to(coef[2 * pairs : 2 * pairs + 1, :], (SUB, LANES))
    factors = [jnp.broadcast_to(coef[i : i + 1, :], (SUB, LANES)) for i in range(2 * pairs)]
    tiles = all_rows // SUB // blocks

    def combine(t, _):
        place = pl.ds(pl.multiple_of(t * SUB, SUB), SUB)
        for lane in range(lat_len // LANES):
            across = pl.ds(lane * LANES, LANES)
            value = ratio * grad[place, across]
            for i in range(pairs):
                value = value + factors[i] * steps[i, place, across]
                value = value + factors[pairs + i] * changes[i, place, across]
            direc[place, across] = value
        return 0

    copies = []
    for block in range(blocks):
        lax.fori_loop(block * tiles, (block + 1) * tiles, combine, 0, unroll=4)
        place = pl.ds(block * tiles * SUB, tiles * SUB)
        copies.append(pltpu.make_async_copy(direc.at[place], dir_hbm.at[place], sems.at[block]))
        copies[-1].start()
    grad_out.wait()
    for copy in copies:
        copy.wait()


def shards(kernels, steps, curvature):
    n_c, n_e = lax.axis_size("cuts"), lax.axis_size("event")
    _, lons, rad_len, lat_len = kernels.shape
    pairs = steps.shape[0]
    part = rad_len // n_e
    assert lons == 2 * RIM and n_e == 4
    all_rows = lons * part
    count = pairs * (pairs + 1)
    f32, bf16 = jnp.float32, jnp.bfloat16
    vmem, dma = pltpu.VMEM, pltpu.SemaphoreType.DMA
    half = (RIM, part, lat_len)
    whole = (2,) + half
    vmem_spec = pl.BlockSpec(memory_space=pltpu.VMEM)
    any_spec = pl.BlockSpec(memory_space=pl.ANY)
    out = jax.ShapeDtypeStruct((all_rows, lat_len), f32)
    others = n_c * n_e - 1
    assert 2 * pairs * SUB == LANES
    staged = pl.pallas_call(
        functools.partial(kernel, (n_c, n_e, pairs, rad_len, lat_len)),
        out_shape=(
            vmem((all_rows, lat_len), f32),
            vmem((pairs, all_rows, lat_len), f32),
            vmem((pairs, all_rows, lat_len), f32),
            vmem((2 * pairs + SUB, LANES), f32),
        ),
        in_specs=[any_spec] * 3,
        out_specs=(vmem_spec,) * 4,
        scratch_shapes=[
            vmem((2, RIM, rad_len, lat_len), f32),
            vmem((2, RIM, rad_len, lat_len), f32),
            vmem(whole, f32),
            vmem(whole, f32),
            vmem(whole, f32),
            vmem(whole, f32),
            vmem(whole, f32),
            vmem(whole, f32),
            vmem((rad_len, 3 * rad_len), bf16),
            vmem((3 * lat_len, lat_len), bf16),
            vmem((count, SUB, LANES), f32),
            vmem((1, LANES), f32),
            vmem((others, 1, LANES), f32),
            vmem((LANES, LANES), f32),
            vmem((LANES, LANES), f32),
            vmem((2 * pairs, LANES), f32),
            vmem((1, LANES), f32),
            vmem((others, 1, LANES), f32),
            dma((RIM + 2,)),
            dma((2, RIM)),
            dma((2, RIM)),
            dma((part // SUB, SPLIT)),
            dma((part // SUB, SPLIT)),
            dma((2, part // SUB, SPLIT)),
            dma((2, part // SUB, SPLIT)),
            dma((others,)),
            dma((others,)),
            dma((others,)),
            dma((others,)),
        ],
        compiler_params=pltpu.CompilerParams(
            collective_id=0, has_side_effects=True, vmem_limit_bytes=61905306
        ),
    )(
        kernels.reshape(2, RIM, rad_len, lat_len),
        steps.reshape(pairs, all_rows, lat_len),
        curvature.reshape(pairs, all_rows, lat_len),
    )
    blocks = 4
    gradient, direction = pl.pallas_call(
        functools.partial(combine_kernel, pairs, blocks),
        out_shape=(out, out),
        in_specs=[vmem_spec] * 4,
        out_specs=(any_spec, any_spec),
        scratch_shapes=[vmem((all_rows, lat_len), f32), dma((blocks + 1,))],
        compiler_params=pltpu.CompilerParams(vmem_limit_bytes=2 * 1024 * 1024),
    )(*staged)
    shape = (lons, part, lat_len)
    return gradient.reshape(shape), direction.reshape(shape)


def solution(mesh):
    placed = (
        P("event", "cuts", None, None),
        P(None, "cuts", "event", None),
        P(None, "cuts", "event", None),
    )
    return jax.shard_map(
        shards,
        mesh=mesh,
        in_specs=placed,
        out_specs=(P("cuts", "event", None), P("cuts", "event", None)),
        check_vma=False,
    )
```

profile of v0, /device:TPU:0, one launch (start us, length us, event | category | flops | bytes accessed | tf_op | source)
XLA Modules:
  0.0 28.6 jit_solution(13814434262770059454)
XLA Ops:
  0.6 26.9 %shard_map.50 = (f32[256,256]{1,0:T(8,128)S(1)}, f32[8,256,256]{2,1,0:T(8,128)S(1)}, f32[8,256,256]{2,1,0:T(8,128)S(1)}, f32[24,128]{1,0:T(8,128)S(1)}) custom-call(f32[2,4,128,256]{3,2,1,0:T(8,128)} %bitcast.7, f32[8,256,256]{2,1,0:T(8,128)} %bitcast.5, f32[8,256,256]{2,1,0:T(8,128)} %bitcast.6), custom_call_target="tpu_custom_call" | custom-call | tf_op jit(solution)/shard_map/pallas_call | solution.py:370
  27.5 1.0 %shard_map.51 = (f32[256,256]{1,0:T(8,128)}, f32[256,256]{1,0:T(8,128)}) custom-call(f32[256,256]{1,0:T(8,128)S(1)} %get-tuple-element.8.grad, f32[8,256,256]{2,1,0:T(8,128)S(1)} %get-tuple-element.9.steps, f32[8,256,256]{2,1,0:T(8,128)S(1)} %get-tuple-element.10.changes, f32[24,128]{1,0:T(8,128)S(1)} %get-tuple-element.11.coef), custom_call_target="tpu_custom_call" | custom-call | tf_op jit(solution)/shard_map/pallas_call | solution.py:420
where the time goes:
time: 28.7 us; the launch traced here: 28.6 us
  Pallas kernels  27.9 us (97%)
  between operations  0.64 us (2%)
    pallas_call x1, Pallas kernels, shards(): pl.pallas_call(functools.partial(kernel, (n_c, n_e, pairs, rad_len, lat_l...  26.9 us
    pallas_call x1, Pallas kernels, shards(): pl.pallas_call(functools.partial(combine_kernel, pairs, blocks), out_shap...  1.05 us

commit v1 on v0

--- a/solution.py
+++ b/solution.py
@@ -9,7 +9,7 @@
 from jax.sharding import PartitionSpec as P
 
 RIM = 4
-SPLIT = 2
+LOADS = 4
 LANES = 128
 SUB = 8
 MESH = pl.DeviceIdType.MESH
@@ -34,6 +34,16 @@
     return jnp.exp(-offset * offset / (2.0 * sigma * sigma))
 
 
+def factor(shape, spot_axis, length, sigma, count):
+    reach = 2.25 * sigma
+    pitch = (length - 1 + 2 * reach) / (count - 1)
+    assert pitch < 0.54 * sigma
+    spots = lax.broadcasted_iota(jnp.int32, shape, spot_axis).astype(jnp.float32)
+    nodes = lax.broadcasted_iota(jnp.int32, shape, 1 - spot_axis).astype(jnp.float32)
+    offset = spots - (nodes * pitch - reach)
+    return jnp.exp(-offset * offset / (sigma * sigma))
+
+
 def upper(pairs):
     return [(i, j) for i in range(pairs) for j in range(i, pairs)]
 
@@ -41,10 +51,10 @@
 def kernel(
     sizes,
     kern_hbm, steps_hbm, curv_hbm, grad, steps, changes, coef,
-    kern, rad, far_in, near_in, far_out, x_in, plane, halo_in,
-    rad_mat, lat_mat, gram_acc, gram_row, gram_all,
+    kern, rad, far_in, near_in, far_out, x_in, nodes, halo_in, smooth, short,
+    rad_mat, pack_mat, dual_mat, lat_mat, gram_acc, gram_row, gram_all,
     table, splat, mix, late_row, late_all,
-    load_sem, core_send, core_recv, x_send, x_recv, halo_send, halo_recv,
+    ready, load_sem, core_send, core_recv, x_send, x_recv, halo_send, halo_recv,
     gram_send, gram_recv, late_send, late_recv,
 ):
     n_c, n_e, pairs, rad_len, lat_len = sizes
@@ -52,27 +62,66 @@
     c = lax.axis_index("cuts")
     e = lax.axis_index("event")
     barrier = pltpu.get_barrier_semaphore()
-    others = [
-        {"cuts": lax.rem(c + d // n_e, n_c), "event": lax.rem(e + d % n_e, n_e)}
-        for d in range(1, n_c * n_e)
-    ]
-    for other in others:
-        pl.semaphore_signal(barrier, 1, device_id=other, device_id_type=MESH)
-
-    loads = [
-        pltpu.make_async_copy(kern_hbm.at[:, k], kern.at[:, k], load_sem.at[k]) for k in range(RIM)
-    ]
-    loads.append(pltpu.make_async_copy(steps_hbm, steps, load_sem.at[RIM]))
-    loads.append(pltpu.make_async_copy(curv_hbm, changes, load_sem.at[RIM + 1]))
-    for load in loads:
-        load.start()
+    steps_left, steps_right = c >= 2, c + 2 < n_c
+    rounds = n_c // 2
+
+    def flip(place):
+        return c + place * (1 - 2 * lax.rem(c // place, 2))
+
+    def greet(semaphore):
+        for d in range(1, n_e):
+            pl.semaphore_signal(
+                semaphore, 1, device_id={"event": lax.rem(e + d, n_e)}, device_id_type=MESH
+            )
+        pl.semaphore_signal(semaphore, 1, device_id={"cuts": flip(1)}, device_id_type=MESH)
+
+        @pl.when(steps_left)
+        def _():
+            pl.semaphore_signal(semaphore, 1, device_id={"cuts": c - 2}, device_id_type=MESH)
+
+        @pl.when(steps_right)
+        def _():
+            pl.semaphore_signal(semaphore, 1, device_id={"cuts": c + 2}, device_id_type=MESH)
+
+    def greeted(semaphore):
+        pl.semaphore_wait(
+            semaphore, n_e + steps_left.astype(jnp.int32) + steps_right.astype(jnp.int32)
+        )
+
+    def relay(number):
+        greeted(ready.at[number - 1] if number else barrier)
+        if number < rounds:
+            greet(ready.at[number])
+
+    greet(barrier)
+    others = []
+    for mask in reversed(range(n_c)):
+        where = c
+        for bit in range(mask.bit_length()):
+            if mask >> bit & 1:
+                where = where + (flip(1 << bit) - c)
+        for d in range(n_e):
+            if mask or d:
+                others.append({"cuts": where, "event": lax.rem(e + d, n_e)})
+
+    per = 2 * RIM // LOADS
+    loads = []
+    for p in range(LOADS):
+        side, ks = p * per // RIM, pl.ds(p * per % RIM, per)
+        loads.append(pltpu.make_async_copy(
+            kern_hbm.at[side, ks], kern.at[side, ks], load_sem.at[p]
+        ))
+        loads[-1].start()
+    loads.append(pltpu.make_async_copy(steps_hbm, steps, load_sem.at[LOADS]))
+    loads.append(pltpu.make_async_copy(curv_hbm, changes, load_sem.at[LOADS + 1]))
 
     matrix = unscaled_gauss(rad_len, 3.0)
     high, low = halves(matrix / jnp.sum(matrix, axis=1, keepdims=True))
     rad_mat[...] = jnp.concatenate([high, high, low], axis=1)
-    matrix = unscaled_gauss(lat_len, 4.0)
-    high, low = halves(matrix / jnp.sum(matrix, axis=0, keepdims=True))
-    lat_mat[...] = jnp.concatenate([high, high, low], axis=0)
+    spread_out = factor((lat_len, LANES), 0, lat_len, 4.0, LANES)
+    high, low = halves(spread_out)
+    both = jnp.concatenate([high, low], axis=1)
+    pack_mat[...] = jnp.concatenate([both, both], axis=0)
     table[...] = jnp.zeros_like(table)
 
     core = e + 1 - 2 * lax.rem(e, 2)
@@ -89,46 +138,67 @@
         )
 
     far_copies, near_copies, x_copies, halo_copies = [], [], [], []
-    for k in range(RIM):
-        loads[k].wait()
-        for side in range(2):
-            high, low = halves(kern[side, k])
-            rad[side, k] = jnp.dot(
-                rad_mat[...], jnp.concatenate([high, low, high], axis=0),
-                preferred_element_type=jnp.float32,
-            )
-    pl.semaphore_wait(barrier, len(others))
-    for k in range(RIM):
-        far_copies.append(send(
-            rad.at[:, k, rows(core_far)], far_in.at[:, k], core_send.at[0, k], core_recv.at[0, k],
-            {"event": core},
-        ))
-        far_copies[-1].start()
-    for k in range(RIM):
-        near_copies.append(send(
-            rad.at[:, k, rows(core)], near_in.at[:, k], core_send.at[1, k], core_recv.at[1, k],
-            {"event": core},
-        ))
-        near_copies[-1].start()
+
+    def packed(value, matrix):
+        high, low = halves(value)
+        out = jnp.dot(
+            jnp.concatenate([high, low], axis=1), matrix[...], preferred_element_type=jnp.float32
+        )
+        return out[:, :LANES] + out[:, LANES:]
+
+    for p in range(LOADS):
+        side, first = p * per // RIM, p * per % RIM
+        loads[p].wait()
+        if p == LOADS - 1:
+            for load in loads[LOADS:]:
+                load.start()
+        value = packed(
+            kern[side, pl.ds(first, per)].reshape(per * rad_len, lat_len), pack_mat
+        ).reshape(per, rad_len, LANES)
+        high, low = halves(jnp.concatenate([value[k] for k in range(per)], axis=1))
+        value = jnp.dot(
+            rad_mat[...], jnp.concatenate([high, low, high], axis=0),
+            preferred_element_type=jnp.float32,
+        )
+        for k in range(per):
+            rad[side, first + k] = value[:, k * LANES : (k + 1) * LANES]
+    relay(0)
+    for number, (copies, chunk, into) in enumerate(
+        ((far_copies, core_far, far_in), (near_copies, core, near_in))
+    ):
+        for p in range(LOADS):
+            side, ks = p * per // RIM, pl.ds(p * per % RIM, per)
+            copies.append(send(
+                rad.at[side, ks, rows(chunk)], into.at[side, ks],
+                core_send.at[number, p], core_recv.at[number, p], {"event": core},
+            ))
+            copies[-1].start()
     strips = part // SUB
-    step_k = RIM // SPLIT
-    pieces = [(h, g) for h in range(strips) for g in range(SPLIT)]
+    pieces = [(h, g) for h in range(strips) for g in range(2)]
 
     def strip_rows(chunk, h):
         return pl.ds(pl.multiple_of(chunk * part + h * SUB, SUB), SUB)
 
+    matrix = spread_out * jnp.sum(spread_out, axis=0, keepdims=True)
+    high, low = halves(spread_out / jnp.sum(matrix, axis=1, keepdims=True))
+    both = jnp.concatenate([high, low], axis=1)
+    dual_mat[...] = jnp.concatenate([both, both], axis=0)
+    matrix = factor((LANES, lat_len), 1, lat_len, 4.0, LANES)
+    whole = jnp.sum(matrix * jnp.sum(matrix, axis=1, keepdims=True), axis=0, keepdims=True)
+    high, low = halves(matrix / whole)
+    lat_mat[...] = jnp.concatenate([high, high, low], axis=0)
+
+    for copy in far_copies:
+        copy.wait_recv()
     for h, g in pieces:
-        ks = pl.ds(g * step_k, step_k)
-        if h == 0:
-            for k in range(g * step_k, (g + 1) * step_k):
-                far_copies[k].wait_recv()
         here = pl.ds(h * SUB, SUB)
-        far_out[:, ks, here] = rad[:, ks, strip_rows(far, h)] + far_in[:, ks, here]
+        far_out[g, :, here] = rad[g, :, strip_rows(far, h)] + far_in[g, :, here]
         x_copies.append(send(
-            far_out.at[:, ks, here], x_in.at[:, ks, here], x_send.at[h, g], x_recv.at[h, g],
+            far_out.at[g, :, here], x_in.at[g, :, here], x_send.at[h, g], x_recv.at[h, g],
             {"event": far},
         ))
         x_copies[-1].start()
+    relay(1)
 
     slots = {pair: number for number, pair in enumerate(upper(pairs))}
     count = len(slots)
@@ -140,8 +210,8 @@
 
     def gram(number):
         if number == 0:
-            loads[RIM].wait()
-            loads[RIM + 1].wait()
+            loads[LOADS].wait()
+            loads[LOADS + 1].wait()
 
         def scale(t, _):
             place = pl.ds(pl.multiple_of(t * SUB, SUB), SUB)
@@ -180,75 +250,67 @@
                         gram_acc[place] = gram_acc[place] + sums[2 * m + kind]
 
     def spread(row, slot_refs, sends, recvs):
-        copies = []
         for d, other in enumerate(others):
-            copies.append(send(row, slot_refs.at[d], sends.at[d], recvs.at[d], other))
-            copies[-1].start()
-        return copies
+            send(row, slot_refs.at[d], sends.at[d], recvs.at[d], other).start()
+        return [
+            send(row, slot_refs.at[d], sends.at[d], recvs.at[d], other)
+            for d, other in enumerate(others)
+        ]
 
     def gathered(row, slot_refs, copies):
         for copy in copies:
             copy.wait_recv()
         return row[...] + jnp.sum(slot_refs[...], axis=0)
 
-    def arrive(h):
+    def arrive(h, g):
         here = pl.ds(h * SUB, SUB)
-        for g in range(SPLIT):
-            ks = pl.ds(g * step_k, step_k)
-            if h == 0:
-                for k in range(g * step_k, (g + 1) * step_k):
-                    near_copies[k].wait_recv()
-            base = rad[:, ks, strip_rows(e, h)] + near_in[:, ks, here]
-            x_copies[h * SPLIT + g].wait_recv()
-            whole = (base + x_in[:, ks, here]).reshape(2 * step_k * SUB, lat_len)
-            high, low = halves(whole)
-            plane[:, ks, here] = jnp.dot(
-                jnp.concatenate([high, low, high], axis=1), lat_mat[...],
-                preferred_element_type=jnp.float32,
-            ).reshape(2, step_k, SUB, lat_len)
-            odd = lax.rem(c, 2)
-            for side in (odd, 1 - odd):
-                halo_copies.append(send(
-                    plane.at[side, ks, here], halo_in.at[side, ks, here],
-                    halo_send.at[side, h, g], halo_recv.at[side, h, g],
-                    {"cuts": lax.rem(c + n_c - 1 + 2 * side, n_c)},
-                ))
-                halo_copies[-1].start()
+        base = rad[g, :, strip_rows(e, h)] + near_in[g, :, here]
+        x_copies[2 * h + g].wait_recv()
+        nodes[g, :, here] = base + x_in[g, :, here]
+        halo_copies.append(send(
+            nodes.at[g, :, here], halo_in.at[g, :, here], halo_send.at[h, g], halo_recv.at[h, g],
+            {"cuts": lax.rem(c + n_c - 1 + 2 * g, n_c)},
+        ))
+        halo_copies[-1].start()
+
+    def shorten(i):
+        for kind, vector in enumerate((steps, changes)):
+            short[kind * pairs + i] = packed(vector[i], dual_mat)
 
     weights = cycle_weights()
     lons = 2 * RIM
 
     def finish(h):
-        for copy in halo_copies[2 * SPLIT * h : 2 * SPLIT * (h + 1)]:
+        for copy in halo_copies[2 * h : 2 * h + 2]:
             copy.wait_recv()
+        place = pl.ds(h * SUB, SUB)
+        padded = (
+            [halo_in[1, k, place] for k in range(RIM)]
+            + [nodes[side, k, place] for side in range(2) for k in range(RIM)]
+            + [halo_in[0, k, place] for k in range(RIM)]
+        )
         sums = [None] * (2 * pairs)
-        for lane in range(lats):
-            place, across = pl.ds(h * SUB, SUB), pl.ds(lane * LANES, LANES)
-            padded = (
-                [halo_in[1, k, place, across] for k in range(RIM)]
-                + [plane[side, k, place, across] for side in range(2) for k in range(RIM)]
-                + [halo_in[0, k, place, across] for k in range(RIM)]
-            )
-            for a in range(lons):
-                value = weights[RIM] * padded[a + RIM]
-                for k in range(1, RIM + 1):
-                    value = value + weights[RIM + k] * (padded[a + RIM - k] + padded[a + RIM + k])
-                spot = pl.ds(a * part + h * SUB, SUB)
-                grad[spot, across] = value
-                for i in range(pairs):
-                    for n, vector in ((i, steps), (pairs + i, changes)):
-                        term = value * vector[i, spot, across]
-                        sums[n] = term if sums[n] is None else sums[n] + term
+        for a in range(lons):
+            value = weights[RIM] * padded[a + RIM]
+            for k in range(1, RIM + 1):
+                value = value + weights[RIM + k] * (padded[a + RIM - k] + padded[a + RIM + k])
+            spot = pl.ds(a * part + h * SUB, SUB)
+            smooth[spot, :] = value
+            for n in range(2 * pairs):
+                term = value * short[n, spot, :]
+                sums[n] = term if sums[n] is None else sums[n] + term
         for n in range(2 * pairs):
             place = pl.ds(n * SUB, SUB)
             table[place, :] = sums[n] if h == 0 else table[place, :] + sums[n]
 
     gram(0)
+    relay(2)
     gram(1)
-    arrive(0)
+    for number in range(3, rounds):
+        relay(number)
     gram(2)
-    arrive(1)
     gram(3)
+    relay(rounds)
     ones = jnp.ones((LANES, LANES), jnp.float32)
 
     def lane_sums(value):
@@ -260,8 +322,12 @@
     table[pl.ds(0, 2 * count), :] = jnp.sum(gram_acc[...], axis=1)
     gram_row[...] = lane_sums(table[...])
     gram_copies = spread(gram_row, gram_all, gram_send, gram_recv)
-    for h in range(2, strips):
-        arrive(h)
+    for copy in near_copies:
+        copy.wait_recv()
+    for number, (h, g) in enumerate(pieces):
+        arrive(h, g)
+        for i in range(number * pairs // len(pieces), (number + 1) * pairs // len(pieces)):
+            shorten(i)
     for h in range(strips):
         finish(h)
     first, _ = halves(table[...])
@@ -271,6 +337,11 @@
         (((1,), (1,)), ((), ())), preferred_element_type=jnp.float32,
     )[:1]
     late_copies = spread(late_row, late_all, late_send, late_recv)
+    high, low = halves(smooth[...])
+    grad[...] = jnp.dot(
+        jnp.concatenate([high, low, high], axis=1), lat_mat[...],
+        preferred_element_type=jnp.float32,
+    )
     products = gathered(gram_row, gram_all, gram_copies)
     square = (LANES, LANES)
     on_diagonal = lax.broadcasted_iota(jnp.int32, square, 0) == lax.broadcasted_iota(jnp.int32, square, 1)
@@ -311,13 +382,13 @@
         mix[i : i + 1, :] = -onto[i]
         mix[pairs + i : pairs + i + 1, :] = scaling * alphas[i]
 
+    for copies in (far_copies, near_copies, x_copies, halo_copies, gram_copies, late_copies):
+        for copy in copies:
+            copy.wait_send()
     products = gathered(late_row, late_all, late_copies)
     mixed = jnp.sum(mix[...] * products, axis=1, keepdims=True)
     coef[pl.ds(0, 2 * pairs), :] = jnp.broadcast_to(mixed, (2 * pairs, LANES))
     coef[pl.ds(2 * pairs, SUB), :] = jnp.broadcast_to(-scaling, (SUB, LANES))
-    for copies in (far_copies, near_copies, x_copies, halo_copies, gram_copies, late_copies):
-        for copy in copies:
-            copy.wait_send()
 
 
 def combine_kernel(pairs, blocks, grad, steps, changes, coef, grad_hbm, dir_hbm, direc, sems):
@@ -355,13 +426,12 @@
     _, lons, rad_len, lat_len = kernels.shape
     pairs = steps.shape[0]
     part = rad_len // n_e
-    assert lons == 2 * RIM and n_e == 4
+    assert lons == 2 * RIM and n_e == 4 and n_c % 2 == 0
     all_rows = lons * part
     count = pairs * (pairs + 1)
     f32, bf16 = jnp.float32, jnp.bfloat16
     vmem, dma = pltpu.VMEM, pltpu.SemaphoreType.DMA
-    half = (RIM, part, lat_len)
-    whole = (2,) + half
+    whole = (2, RIM, part, LANES)
     vmem_spec = pl.BlockSpec(memory_space=pltpu.VMEM)
     any_spec = pl.BlockSpec(memory_space=pl.ANY)
     out = jax.ShapeDtypeStruct((all_rows, lat_len), f32)
@@ -379,15 +449,19 @@
         out_specs=(vmem_spec,) * 4,
         scratch_shapes=[
             vmem((2, RIM, rad_len, lat_len), f32),
-            vmem((2, RIM, rad_len, lat_len), f32),
+            vmem((2, RIM, rad_len, LANES), f32),
             vmem(whole, f32),
             vmem(whole, f32),
             vmem(whole, f32),
             vmem(whole, f32),
             vmem(whole, f32),
             vmem(whole, f32),
+            vmem((all_rows, LANES), f32),
+            vmem((2 * pairs, all_rows, LANES), f32),
             vmem((rad_len, 3 * rad_len), bf16),
-            vmem((3 * lat_len, lat_len), bf16),
+            vmem((2 * lat_len, 2 * LANES), bf16),
+            vmem((2 * lat_len, 2 * LANES), bf16),
+            vmem((3 * LANES, lat_len), bf16),
             vmem((count, SUB, LANES), f32),
             vmem((1, LANES), f32),
             vmem((others, 1, LANES), f32),
@@ -396,13 +470,14 @@
             vmem((2 * pairs, LANES), f32),
             vmem((1, LANES), f32),
             vmem((others, 1, LANES), f32),
-            dma((RIM + 2,)),
-            dma((2, RIM)),
-            dma((2, RIM)),
-            dma((part // SUB, SPLIT)),
-            dma((part // SUB, SPLIT)),
-            dma((2, part // SUB, SPLIT)),
-            dma((2, part // SUB, SPLIT)),
+            pltpu.SemaphoreType.REGULAR((n_c // 2,)),
+            dma((LOADS + 2,)),
+            dma((2, LOADS)),
+            dma((2, LOADS)),
+            dma((part // SUB, 2)),
+            dma((part // SUB, 2)),
+            dma((part // SUB, 2)),
+            dma((part // SUB, 2)),
             dma((others,)),
             dma((others,)),
             dma((others,)),

time: 28.7 us -> 25.9 us (0.902)
  Pallas kernels: 27.9 us -> 25.1 us
    pallas_call x1, Pallas kernels: 26.9 us -> 24.1 us  [shards(): pl.pallas_call(functools.partial(kernel, (n_c, n_e, pairs, rad_len, lat_l...]
where the time goes in v1:
time: 25.9 us; the launch traced here: 25.8 us
  Pallas kernels  25.1 us (97%)
  between operations  0.64 us (2%)
    pallas_call x1, Pallas kernels, shards(): pl.pallas_call(functools.partial(kernel, (n_c, n_e, pairs, rad_len, lat_l...  24.1 us
    pallas_call x1, Pallas kernels, shards(): pl.pallas_call(functools.partial(combine_kernel, pairs, blocks), out_shap...  1.05 us

profile of v1, /device:TPU:0, one launch (start us, length us, event | category | flops | bytes accessed | tf_op | source)
XLA Modules:
  0.0 25.8 jit_solution(14811952653800925854)
XLA Ops:
  0.6 24.1 %shard_map.50 = (f32[256,256]{1,0:T(8,128)S(1)}, f32[8,256,256]{2,1,0:T(8,128)S(1)}, f32[8,256,256]{2,1,0:T(8,128)S(1)}, f32[24,128]{1,0:T(8,128)S(1)}) custom-call(f32[2,4,128,256]{3,2,1,0:T(8,128)} %bitcast.7, f32[8,256,256]{2,1,0:T(8,128)} %bitcast.5, f32[8,256,256]{2,1,0:T(8,128)} %bitcast.6), custom_call_target="tpu_custom_call" | custom-call | tf_op jit(solution)/shard_map/pallas_call | solution.py:440
  24.7 1.0 %shard_map.51 = (f32[256,256]{1,0:T(8,128)}, f32[256,256]{1,0:T(8,128)}) custom-call(f32[256,256]{1,0:T(8,128)S(1)} %get-tuple-element.8.grad, f32[8,256,256]{2,1,0:T(8,128)S(1)} %get-tuple-element.9.steps, f32[8,256,256]{2,1,0:T(8,128)S(1)} %get-tuple-element.10.changes, f32[24,128]{1,0:T(8,128)S(1)} %get-tuple-element.11.coef), custom_call_target="tpu_custom_call" | custom-call | tf_op jit(solution)/shard_map/pallas_call | solution.py:495

commit v2 on v1

--- a/solution.py
+++ b/solution.py
@@ -50,14 +50,15 @@
 
 def kernel(
     sizes,
-    kern_hbm, steps_hbm, curv_hbm, grad, steps, changes, coef,
-    kern, rad, far_in, near_in, far_out, x_in, nodes, halo_in, smooth, short,
+    kern_hbm, steps_hbm, curv_hbm, out,
+    steps, changes, kern, rad, far_in, near_in, far_out, x_in, nodes, halo_in, smooth, short,
     rad_mat, pack_mat, dual_mat, lat_mat, gram_acc, gram_row, gram_all,
     table, splat, mix, late_row, late_all,
     ready, load_sem, core_send, core_recv, x_send, x_recv, halo_send, halo_recv,
     gram_send, gram_recv, late_send, late_recv,
 ):
     n_c, n_e, pairs, rad_len, lat_len = sizes
+    grad, direc = out.at[0], out.at[1]
     part = rad_len // n_e
     c = lax.axis_index("cuts")
     e = lax.axis_index("event")
@@ -174,7 +175,8 @@
             ))
             copies[-1].start()
     strips = part // SUB
-    pieces = [(h, g) for h in range(strips) for g in range(2)]
+    sides = (lax.rem(c, 2), 1 - lax.rem(c, 2))
+    pieces = [(h, turn) for turn in range(2) for h in range(strips)]
 
     def strip_rows(chunk, h):
         return pl.ds(pl.multiple_of(chunk * part + h * SUB, SUB), SUB)
@@ -190,11 +192,11 @@
 
     for copy in far_copies:
         copy.wait_recv()
-    for h, g in pieces:
-        here = pl.ds(h * SUB, SUB)
+    for h, turn in pieces:
+        here, g = pl.ds(h * SUB, SUB), sides[turn]
         far_out[g, :, here] = rad[g, :, strip_rows(far, h)] + far_in[g, :, here]
         x_copies.append(send(
-            far_out.at[g, :, here], x_in.at[g, :, here], x_send.at[h, g], x_recv.at[h, g],
+            far_out.at[g, :, here], x_in.at[g, :, here], x_send.at[h, turn], x_recv.at[h, turn],
             {"event": far},
         ))
         x_copies[-1].start()
@@ -262,10 +264,11 @@
             copy.wait_recv()
         return row[...] + jnp.sum(slot_refs[...], axis=0)
 
-    def arrive(h, g):
-        here = pl.ds(h * SUB, SUB)
+    def arrive(number):
+        h, turn = pieces[number]
+        here, g = pl.ds(h * SUB, SUB), sides[turn]
         base = rad[g, :, strip_rows(e, h)] + near_in[g, :, here]
-        x_copies[2 * h + g].wait_recv()
+        x_copies[number].wait_recv()
         nodes[g, :, here] = base + x_in[g, :, here]
         halo_copies.append(send(
             nodes.at[g, :, here], halo_in.at[g, :, here], halo_send.at[h, g], halo_recv.at[h, g],
@@ -273,15 +276,15 @@
         ))
         halo_copies[-1].start()
 
-    def shorten(i):
-        for kind, vector in enumerate((steps, changes)):
+    def shorten(kind, vector):
+        for i in range(pairs):
             short[kind * pairs + i] = packed(vector[i], dual_mat)
 
     weights = cycle_weights()
     lons = 2 * RIM
 
     def finish(h):
-        for copy in halo_copies[2 * h : 2 * h + 2]:
+        for copy in halo_copies[h::strips]:
             copy.wait_recv()
         place = pl.ds(h * SUB, SUB)
         padded = (
@@ -305,12 +308,17 @@
 
     gram(0)
     relay(2)
-    gram(1)
+    shorten(0, steps)
     for number in range(3, rounds):
         relay(number)
+    gram(1)
+    for copy in near_copies:
+        copy.wait_recv()
+    for number in range(len(pieces)):
+        arrive(number)
+    relay(rounds)
     gram(2)
     gram(3)
-    relay(rounds)
     ones = jnp.ones((LANES, LANES), jnp.float32)
 
     def lane_sums(value):
@@ -322,12 +330,7 @@
     table[pl.ds(0, 2 * count), :] = jnp.sum(gram_acc[...], axis=1)
     gram_row[...] = lane_sums(table[...])
     gram_copies = spread(gram_row, gram_all, gram_send, gram_recv)
-    for copy in near_copies:
-        copy.wait_recv()
-    for number, (h, g) in enumerate(pieces):
-        arrive(h, g)
-        for i in range(number * pairs // len(pieces), (number + 1) * pairs // len(pieces)):
-            shorten(i)
+    shorten(1, changes)
     for h in range(strips):
         finish(h)
     first, _ = halves(table[...])
@@ -387,21 +390,14 @@
             copy.wait_send()
     products = gathered(late_row, late_all, late_copies)
     mixed = jnp.sum(mix[...] * products, axis=1, keepdims=True)
-    coef[pl.ds(0, 2 * pairs), :] = jnp.broadcast_to(mixed, (2 * pairs, LANES))
-    coef[pl.ds(2 * pairs, SUB), :] = jnp.broadcast_to(-scaling, (SUB, LANES))
-
-
-def combine_kernel(pairs, blocks, grad, steps, changes, coef, grad_hbm, dir_hbm, direc, sems):
-    grad_out = pltpu.make_async_copy(grad, grad_hbm, sems.at[blocks])
-    grad_out.start()
-    all_rows, lat_len = grad.shape
-    ratio = jnp.broadcast_to(coef[2 * pairs : 2 * pairs + 1, :], (SUB, LANES))
-    factors = [jnp.broadcast_to(coef[i : i + 1, :], (SUB, LANES)) for i in range(2 * pairs)]
-    tiles = all_rows // SUB // blocks
+    factors = [
+        jnp.broadcast_to(mixed[i : i + 1], (SUB, LANES)) for i in range(2 * pairs)
+    ]
+    ratio = jnp.broadcast_to(-scaling, (SUB, LANES))
 
     def combine(t, _):
         place = pl.ds(pl.multiple_of(t * SUB, SUB), SUB)
-        for lane in range(lat_len // LANES):
+        for lane in range(lats):
             across = pl.ds(lane * LANES, LANES)
             value = ratio * grad[place, across]
             for i in range(pairs):
@@ -410,15 +406,7 @@
             direc[place, across] = value
         return 0
 
-    copies = []
-    for block in range(blocks):
-        lax.fori_loop(block * tiles, (block + 1) * tiles, combine, 0, unroll=4)
-        place = pl.ds(block * tiles * SUB, tiles * SUB)
-        copies.append(pltpu.make_async_copy(direc.at[place], dir_hbm.at[place], sems.at[block]))
-        copies[-1].start()
-    grad_out.wait()
-    for copy in copies:
-        copy.wait()
+    lax.fori_loop(0, tiles, combine, 0, unroll=4)
 
 
 def shards(kernels, steps, curvature):
@@ -434,20 +422,16 @@
     whole = (2, RIM, part, LANES)
     vmem_spec = pl.BlockSpec(memory_space=pltpu.VMEM)
     any_spec = pl.BlockSpec(memory_space=pl.ANY)
-    out = jax.ShapeDtypeStruct((all_rows, lat_len), f32)
     others = n_c * n_e - 1
     assert 2 * pairs * SUB == LANES
-    staged = pl.pallas_call(
+    outs = pl.pallas_call(
         functools.partial(kernel, (n_c, n_e, pairs, rad_len, lat_len)),
-        out_shape=(
-            vmem((all_rows, lat_len), f32),
+        out_shape=vmem((2, all_rows, lat_len), f32),
+        in_specs=[any_spec] * 3,
+        out_specs=vmem_spec,
+        scratch_shapes=[
             vmem((pairs, all_rows, lat_len), f32),
             vmem((pairs, all_rows, lat_len), f32),
-            vmem((2 * pairs + SUB, LANES), f32),
-        ),
-        in_specs=[any_spec] * 3,
-        out_specs=(vmem_spec,) * 4,
-        scratch_shapes=[
             vmem((2, RIM, rad_len, lat_len), f32),
             vmem((2, RIM, rad_len, LANES), f32),
             vmem(whole, f32),
@@ -491,17 +475,8 @@
         steps.reshape(pairs, all_rows, lat_len),
         curvature.reshape(pairs, all_rows, lat_len),
     )
-    blocks = 4
-    gradient, direction = pl.pallas_call(
-        functools.partial(combine_kernel, pairs, blocks),
-        out_shape=(out, out),
-        in_specs=[vmem_spec] * 4,
-        out_specs=(any_spec, any_spec),
-        scratch_shapes=[vmem((all_rows, lat_len), f32), dma((blocks + 1,))],
-        compiler_params=pltpu.CompilerParams(vmem_limit_bytes=2 * 1024 * 1024),
-    )(*staged)
     shape = (lons, part, lat_len)
-    return gradient.reshape(shape), direction.reshape(shape)
+    return outs[0].reshape(shape), outs[1].reshape(shape)
 
 
 def solution(mesh):

time: 25.9 us -> 24.3 us (0.938)
  Pallas kernels: 25.1 us -> 22.6 us
  local copies, waits for them, and re-layouts: 0 us -> 0.82 us
    pallas_call x1, Pallas kernels: 24.1 us -> 22.6 us  [shards(): pl.pallas_call(functools.partial(kernel, (n_c, n_e, pairs, rad_len, lat_l...]
    pallas_call x1 -> x0, Pallas kernels: 1.05 us -> none  [shards(): pl.pallas_call(functools.partial(combine_kernel, pairs, blocks), out_shap...]
    slice x0 -> x1, local copies, waits for them, and re-layouts: none -> 0.82 us  [shards(): return (outs[0].reshape(shape), outs[1].reshape(shape))]
where the time goes in v2:
time: 24.3 us; the launch traced here: 24.1 us
  Pallas kernels  22.6 us (93%)
  local copies, waits for them, and re-layouts  0.82 us (3%)
  between operations  0.64 us (3%)
    pallas_call x1, Pallas kernels, shards(): pl.pallas_call(functools.partial(kernel, (n_c, n_e, pairs, rad_len, lat_l...  22.6 us
    slice x1, local copies, waits for them, and re-layouts, shards(): return (outs[0].reshape(shape), outs[1].reshape(shape))  0.82 us

profile of v2, /device:TPU:0, one launch (start us, length us, event | category | flops | bytes accessed | tf_op | source)
XLA Modules:
  0.0 24.1 jit_solution(16633655690264906292)
XLA Ops:
  0.6 22.6 %shard_map.50 = f32[2,256,256]{2,1,0:T(8,128)S(1)} custom-call(f32[2,4,128,256]{3,2,1,0:T(8,128)} %bitcast.7, f32[8,256,256]{2,1,0:T(8,128)} %bitcast.5, f32[8,256,256]{2,1,0:T(8,128)} %bitcast.6), custom_call_target="tpu_custom_call" | custom-call | tf_op jit(solution)/shard_map/pallas_call | solution.py:427
  23.3 0.8 %fusion = (f32[1,256,256]{2,1,0:T(8,128)}, f32[1,256,256]{2,1,0:T(8,128)}) fusion(f32[2,256,256]{2,1,0:T(8,128)S(1)} %shard_map.50), kind=kLoop, calls=%fused_computation | loop fusion | bytes 1048576 | tf_op jit(solution)/shard_map/slice | solution.py:479

commit v3 on v2

--- a/solution.py
+++ b/solution.py
@@ -64,37 +64,64 @@
     e = lax.axis_index("event")
     barrier = pltpu.get_barrier_semaphore()
     steps_left, steps_right = c >= 2, c + 2 < n_c
-    rounds = n_c // 2
 
     def flip(place):
         return c + place * (1 - 2 * lax.rem(c // place, 2))
 
-    def greet(semaphore):
-        for d in range(1, n_e):
-            pl.semaphore_signal(
-                semaphore, 1, device_id={"event": lax.rem(e + d, n_e)}, device_id_type=MESH
-            )
-        pl.semaphore_signal(semaphore, 1, device_id={"cuts": flip(1)}, device_id_type=MESH)
-
+    def signal(semaphore, **where):
+        pl.semaphore_signal(semaphore, 1, device_id=where, device_id_type=MESH)
+
+    for d in range(1, n_e):
+        signal(barrier, event=lax.rem(e + d, n_e))
+    signal(barrier, cuts=flip(1))
+
+    @pl.when(steps_left)
+    def _():
+        signal(barrier, cuts=c - 2)
+
+    @pl.when(steps_right)
+    def _():
+        signal(barrier, cuts=c + 2)
+
+    def enter():
+        pl.semaphore_wait(barrier, n_e + steps_left.astype(jnp.int32) + steps_right.astype(jnp.int32))
+
+        @pl.when(jnp.logical_not(steps_left) & steps_right)
+        def _():
+            signal(ready.at[0], cuts=c + 2)
+
+        @pl.when(jnp.logical_not(steps_right) & steps_left)
+        def _():
+            signal(ready.at[1], cuts=c - 2)
+
+    def pass_right():
         @pl.when(steps_left)
         def _():
-            pl.semaphore_signal(semaphore, 1, device_id={"cuts": c - 2}, device_id_type=MESH)
-
-        @pl.when(steps_right)
+            pl.semaphore_wait(ready.at[0], 1)
+
+            @pl.when(steps_right)
+            def _():
+                signal(ready.at[0], cuts=c + 2)
+
+    def pass_left():
+        @pl.when(steps_left)
         def _():
-            pl.semaphore_signal(semaphore, 1, device_id={"cuts": c + 2}, device_id_type=MESH)
-
-    def greeted(semaphore):
-        pl.semaphore_wait(
-            semaphore, n_e + steps_left.astype(jnp.int32) + steps_right.astype(jnp.int32)
-        )
-
-    def relay(number):
-        greeted(ready.at[number - 1] if number else barrier)
-        if number < rounds:
-            greet(ready.at[number])
-
-    greet(barrier)
+            @pl.when(steps_right)
+            def _():
+                pl.semaphore_wait(ready.at[1], 1)
+                signal(ready.at[1], cuts=c - 2)
+
+            signal(ready.at[2], cuts=flip(1))
+
+    def end_left():
+        @pl.when(jnp.logical_not(steps_left))
+        def _():
+            @pl.when(steps_right)
+            def _():
+                pl.semaphore_wait(ready.at[1], 1)
+
+            signal(ready.at[2], cuts=flip(1))
+
     others = []
     for mask in reversed(range(n_c)):
         where = c
@@ -105,13 +132,13 @@
             if mask or d:
                 others.append({"cuts": where, "event": lax.rem(e + d, n_e)})
 
+    sides = (lax.rem(c, 2), 1 - lax.rem(c, 2))
     per = 2 * RIM // LOADS
+    chunks = [(sides[p * per // RIM], p * per % RIM) for p in range(LOADS)]
     loads = []
-    for p in range(LOADS):
-        side, ks = p * per // RIM, pl.ds(p * per % RIM, per)
-        loads.append(pltpu.make_async_copy(
-            kern_hbm.at[side, ks], kern.at[side, ks], load_sem.at[p]
-        ))
+    for p, (g, first) in enumerate(chunks):
+        ks = pl.ds(first, per)
+        loads.append(pltpu.make_async_copy(kern_hbm.at[g, ks], kern.at[g, ks], load_sem.at[p]))
         loads[-1].start()
     loads.append(pltpu.make_async_copy(steps_hbm, steps, load_sem.at[LOADS]))
     loads.append(pltpu.make_async_copy(curv_hbm, changes, load_sem.at[LOADS + 1]))
@@ -147,39 +174,45 @@
         )
         return out[:, :LANES] + out[:, LANES:]
 
-    for p in range(LOADS):
-        side, first = p * per // RIM, p * per % RIM
-        loads[p].wait()
-        if p == LOADS - 1:
-            for load in loads[LOADS:]:
-                load.start()
-        value = packed(
-            kern[side, pl.ds(first, per)].reshape(per * rad_len, lat_len), pack_mat
-        ).reshape(per, rad_len, LANES)
-        high, low = halves(jnp.concatenate([value[k] for k in range(per)], axis=1))
-        value = jnp.dot(
-            rad_mat[...], jnp.concatenate([high, low, high], axis=0),
-            preferred_element_type=jnp.float32,
-        )
-        for k in range(per):
-            rad[side, first + k] = value[:, k * LANES : (k + 1) * LANES]
-    relay(0)
-    for number, (copies, chunk, into) in enumerate(
-        ((far_copies, core_far, far_in), (near_copies, core, near_in))
-    ):
-        for p in range(LOADS):
-            side, ks = p * per // RIM, pl.ds(p * per % RIM, per)
+    def exchange(p):
+        g, first = chunks[p]
+        ks = pl.ds(first, per)
+        for number, (copies, chunk, into) in enumerate(
+            ((far_copies, core_far, far_in), (near_copies, core, near_in))
+        ):
             copies.append(send(
-                rad.at[side, ks, rows(chunk)], into.at[side, ks],
+                rad.at[g, ks, rows(chunk)], into.at[g, ks],
                 core_send.at[number, p], core_recv.at[number, p], {"event": core},
             ))
             copies[-1].start()
+
+    value = None
+    for p in range(LOADS + 1):
+        before = value
+        if p < LOADS:
+            g, first = chunks[p]
+            loads[p].wait()
+            if p == LOADS - 1:
+                for load in loads[LOADS:]:
+                    load.start()
+            value = packed(
+                kern[g, pl.ds(first, per)].reshape(per * rad_len, lat_len), pack_mat
+            ).reshape(per, rad_len, LANES)
+        if p:
+            high, low = halves(jnp.concatenate([before[k] for k in range(per)], axis=1))
+            done = jnp.dot(
+                rad_mat[...], jnp.concatenate([high, low, high], axis=0),
+                preferred_element_type=jnp.float32,
+            )
+            g, first = chunks[p - 1]
+            for k in range(per):
+                rad[g, first + k] = done[:, k * LANES : (k + 1) * LANES]
+            if p == 2:
+                enter()
+                exchange(0)
+            if p >= 2:
+                exchange(p - 1)
     strips = part // SUB
-    sides = (lax.rem(c, 2), 1 - lax.rem(c, 2))
-    pieces = [(h, turn) for turn in range(2) for h in range(strips)]
-
-    def strip_rows(chunk, h):
-        return pl.ds(pl.multiple_of(chunk * part + h * SUB, SUB), SUB)
 
     matrix = spread_out * jnp.sum(spread_out, axis=0, keepdims=True)
     high, low = halves(spread_out / jnp.sum(matrix, axis=1, keepdims=True))
@@ -190,17 +223,15 @@
     high, low = halves(matrix / whole)
     lat_mat[...] = jnp.concatenate([high, high, low], axis=0)
 
-    for copy in far_copies:
-        copy.wait_recv()
-    for h, turn in pieces:
-        here, g = pl.ds(h * SUB, SUB), sides[turn]
-        far_out[g, :, here] = rad[g, :, strip_rows(far, h)] + far_in[g, :, here]
+    for p, (g, first) in enumerate(chunks):
+        ks = pl.ds(first, per)
+        far_copies[p].wait_recv()
+        far_out[g, ks] = rad[g, ks, rows(far)] + far_in[g, ks]
         x_copies.append(send(
-            far_out.at[g, :, here], x_in.at[g, :, here], x_send.at[h, turn], x_recv.at[h, turn],
-            {"event": far},
+            far_out.at[g, ks], x_in.at[g, ks], x_send.at[p], x_recv.at[p], {"event": far}
         ))
         x_copies[-1].start()
-    relay(1)
+    pass_right()
 
     slots = {pair: number for number, pair in enumerate(upper(pairs))}
     count = len(slots)
@@ -264,61 +295,63 @@
             copy.wait_recv()
         return row[...] + jnp.sum(slot_refs[...], axis=0)
 
-    def arrive(number):
-        h, turn = pieces[number]
-        here, g = pl.ds(h * SUB, SUB), sides[turn]
-        base = rad[g, :, strip_rows(e, h)] + near_in[g, :, here]
-        x_copies[number].wait_recv()
-        nodes[g, :, here] = base + x_in[g, :, here]
+    def arrive(p):
+        g, first = chunks[p]
+        ks = pl.ds(first, per)
+        near_copies[p].wait_recv()
+        base = rad[g, ks, rows(e)] + near_in[g, ks]
+        x_copies[p].wait_recv()
+        nodes[g, ks] = base + x_in[g, ks]
         halo_copies.append(send(
-            nodes.at[g, :, here], halo_in.at[g, :, here], halo_send.at[h, g], halo_recv.at[h, g],
+            nodes.at[g, ks], halo_in.at[g, ks], halo_send.at[p], halo_recv.at[g, first // per],
             {"cuts": lax.rem(c + n_c - 1 + 2 * g, n_c)},
         ))
         halo_copies[-1].start()
 
-    def shorten(kind, vector):
-        for i in range(pairs):
+    def shorten(kind, vector, first, last):
+        for i in range(first, last):
             short[kind * pairs + i] = packed(vector[i], dual_mat)
 
     weights = cycle_weights()
-    lons = 2 * RIM
-
-    def finish(h):
-        for copy in halo_copies[h::strips]:
-            copy.wait_recv()
-        place = pl.ds(h * SUB, SUB)
-        padded = (
-            [halo_in[1, k, place] for k in range(RIM)]
-            + [nodes[side, k, place] for side in range(2) for k in range(RIM)]
-            + [halo_in[0, k, place] for k in range(RIM)]
-        )
+
+    def finish(turn):
+        g = sides[turn]
+        for p in range(turn * LOADS // 2, (turn + 1) * LOADS // 2):
+            first = chunks[p][1]
+            ks = pl.ds(first, per)
+            send(
+                nodes.at[1 - g, ks], halo_in.at[1 - g, ks], halo_send.at[p],
+                halo_recv.at[1 - g, first // per], {"event": core},
+            ).wait_recv()
+
+        def at(k):
+            return k + g * (RIM - 1 - 2 * k)
+
         sums = [None] * (2 * pairs)
-        for a in range(lons):
-            value = weights[RIM] * padded[a + RIM]
-            for k in range(1, RIM + 1):
-                value = value + weights[RIM + k] * (padded[a + RIM - k] + padded[a + RIM + k])
-            spot = pl.ds(a * part + h * SUB, SUB)
-            smooth[spot, :] = value
-            for n in range(2 * pairs):
-                term = value * short[n, spot, :]
-                sums[n] = term if sums[n] is None else sums[n] + term
+        for h in range(strips):
+            place = pl.ds(h * SUB, SUB)
+            padded = (
+                [halo_in[1 - g, at(k), place] for k in range(RIM)]
+                + [nodes[g, at(k), place] for k in range(RIM)]
+                + [nodes[1 - g, at(k), place] for k in range(RIM)]
+            )
+            for a in range(RIM):
+                value = weights[RIM] * padded[a + RIM]
+                for k in range(1, RIM + 1):
+                    value = value + weights[RIM + k] * (padded[a + RIM - k] + padded[a + RIM + k])
+                spot = pl.ds(pl.multiple_of((g * RIM + at(a)) * part + h * SUB, SUB), SUB)
+                smooth[spot, :] = value
+                for n in range(2 * pairs):
+                    term = value * short[n, spot, :]
+                    sums[n] = term if sums[n] is None else sums[n] + term
         for n in range(2 * pairs):
             place = pl.ds(n * SUB, SUB)
-            table[place, :] = sums[n] if h == 0 else table[place, :] + sums[n]
-
-    gram(0)
-    relay(2)
-    shorten(0, steps)
-    for number in range(3, rounds):
-        relay(number)
-    gram(1)
-    for copy in near_copies:
-        copy.wait_recv()
-    for number in range(len(pieces)):
-        arrive(number)
-    relay(rounds)
-    gram(2)
-    gram(3)
+            table[place, :] = sums[n] if turn == 0 else table[place, :] + sums[n]
+
+    pass_left()
+    for number in range(RIM):
+        gram(number)
+    end_left()
     ones = jnp.ones((LANES, LANES), jnp.float32)
 
     def lane_sums(value):
@@ -329,10 +362,14 @@
 
     table[pl.ds(0, 2 * count), :] = jnp.sum(gram_acc[...], axis=1)
     gram_row[...] = lane_sums(table[...])
+    for p in range(LOADS):
+        arrive(p)
+        shorten(0, steps, p * pairs // LOADS, (p + 1) * pairs // LOADS)
+    pl.semaphore_wait(ready.at[2], 1)
     gram_copies = spread(gram_row, gram_all, gram_send, gram_recv)
-    shorten(1, changes)
-    for h in range(strips):
-        finish(h)
+    shorten(1, changes, 0, pairs)
+    finish(0)
+    finish(1)
     first, _ = halves(table[...])
     second, third = halves(table[...] - first.astype(jnp.float32))
     late_row[...] = lax.dot_general(
@@ -399,11 +436,14 @@
         place = pl.ds(pl.multiple_of(t * SUB, SUB), SUB)
         for lane in range(lats):
             across = pl.ds(lane * LANES, LANES)
-            value = ratio * grad[place, across]
+            values = [ratio * grad[place, across]]
             for i in range(pairs):
-                value = value + factors[i] * steps[i, place, across]
-                value = value + factors[pairs + i] * changes[i, place, across]
-            direc[place, across] = value
+                values.append(factors[i] * steps[i, place, across])
+                values.append(factors[pairs + i] * changes[i, place, across])
+            while len(values) > 1:
+                paired = [x + y for x, y in zip(values[::2], values[1::2])]
+                values = paired + values[2 * len(paired) :]
+            direc[place, across] = values[0]
         return 0
 
     lax.fori_loop(0, tiles, combine, 0, unroll=4)
@@ -454,14 +494,14 @@
             vmem((2 * pairs, LANES), f32),
             vmem((1, LANES), f32),
             vmem((others, 1, LANES), f32),
-            pltpu.SemaphoreType.REGULAR((n_c // 2,)),
+            pltpu.SemaphoreType.REGULAR((3,)),
             dma((LOADS + 2,)),
             dma((2, LOADS)),
             dma((2, LOADS)),
-            dma((part // SUB, 2)),
-            dma((part // SUB, 2)),
-            dma((part // SUB, 2)),
-            dma((part // SUB, 2)),
+            dma((LOADS,)),
+            dma((LOADS,)),
+            dma((LOADS,)),
+            dma((2, LOADS // 2)),
             dma((others,)),
             dma((others,)),
             dma((others,)),

time: 24.3 us -> 23.9 us (0.984)
  Pallas kernels: 22.6 us -> 22.2 us
    pallas_call x1, Pallas kernels: 22.6 us -> 22.2 us  [shards(): pl.pallas_call(functools.partial(kernel, (n_c, n_e, pairs, rad_len, lat_l...]
where the time goes in v3:
time: 23.9 us; the launch traced here: 23.7 us
  Pallas kernels  22.2 us (93%)
  local copies, waits for them, and re-layouts  0.82 us (3%)
  between operations  0.64 us (3%)
    pallas_call x1, Pallas kernels, shards(): pl.pallas_call(functools.partial(kernel, (n_c, n_e, pairs, rad_len, lat_l...  22.2 us
    slice x1, local copies, waits for them, and re-layouts, shards(): return (outs[0].reshape(shape), outs[1].reshape(shape))  0.82 us

profile of v3, /device:TPU:0, one launch (start us, length us, event | category | flops | bytes accessed | tf_op | source)
XLA Modules:
  0.0 23.7 jit_solution(8319093540217202007)
XLA Ops:
  0.6 22.2 %shard_map.50 = f32[2,256,256]{2,1,0:T(8,128)S(1)} custom-call(f32[2,4,128,256]{3,2,1,0:T(8,128)} %bitcast.7, f32[8,256,256]{2,1,0:T(8,128)} %bitcast.5, f32[8,256,256]{2,1,0:T(8,128)} %bitcast.6), custom_call_target="tpu_custom_call" | custom-call | tf_op jit(solution)/shard_map/pallas_call | solution.py:467
  22.9 0.8 %fusion = (f32[1,256,256]{2,1,0:T(8,128)}, f32[1,256,256]{2,1,0:T(8,128)}) fusion(f32[2,256,256]{2,1,0:T(8,128)S(1)} %shard_map.50), kind=kLoop, calls=%fused_computation | loop fusion | bytes 1048576 | tf_op jit(solution)/shard_map/slice | solution.py:519

commit v4 on v3

--- a/solution.py
+++ b/solution.py
@@ -51,7 +51,7 @@
 def kernel(
     sizes,
     kern_hbm, steps_hbm, curv_hbm, out,
-    steps, changes, kern, rad, far_in, near_in, far_out, x_in, nodes, halo_in, smooth, short,
+    steps, changes, kern, rad, far_in, near_in, far_out, x_in, cross_in, nodes, halo_in, smooth, short,
     rad_mat, pack_mat, dual_mat, lat_mat, gram_acc, gram_row, gram_all,
     table, splat, mix, late_row, late_all,
     ready, load_sem, core_send, core_recv, x_send, x_recv, halo_send, halo_recv,
@@ -177,14 +177,22 @@
     def exchange(p):
         g, first = chunks[p]
         ks = pl.ds(first, per)
+        if p == 0:
+            for number, (where, into) in enumerate(((far, x_in.at[g, ks]), (core_far, cross_in))):
+                x_copies.append(send(
+                    rad.at[g, ks, rows(where)], into, x_send.at[number], x_recv.at[number],
+                    {"event": where},
+                ))
+                x_copies[-1].start()
         for number, (copies, chunk, into) in enumerate(
             ((far_copies, core_far, far_in), (near_copies, core, near_in))
         ):
-            copies.append(send(
-                rad.at[g, ks, rows(chunk)], into.at[g, ks],
-                core_send.at[number, p], core_recv.at[number, p], {"event": core},
-            ))
-            copies[-1].start()
+            if p or number:
+                copies.append(send(
+                    rad.at[g, ks, rows(chunk)], into.at[g, ks],
+                    core_send.at[number, p], core_recv.at[number, p], {"event": core},
+                ))
+                copies[-1].start()
 
     value = None
     for p in range(LOADS + 1):
@@ -207,11 +215,9 @@
             g, first = chunks[p - 1]
             for k in range(per):
                 rad[g, first + k] = done[:, k * LANES : (k + 1) * LANES]
-            if p == 2:
+            if p == 1:
                 enter()
-                exchange(0)
-            if p >= 2:
-                exchange(p - 1)
+            exchange(p - 1)
     strips = part // SUB
 
     matrix = spread_out * jnp.sum(spread_out, axis=0, keepdims=True)
@@ -223,12 +229,14 @@
     high, low = halves(matrix / whole)
     lat_mat[...] = jnp.concatenate([high, high, low], axis=0)
 
-    for p, (g, first) in enumerate(chunks):
+    for copy, p in zip(far_copies, range(1, LOADS)):
+        g, first = chunks[p]
         ks = pl.ds(first, per)
-        far_copies[p].wait_recv()
+        copy.wait_recv()
         far_out[g, ks] = rad[g, ks, rows(far)] + far_in[g, ks]
         x_copies.append(send(
-            far_out.at[g, ks], x_in.at[g, ks], x_send.at[p], x_recv.at[p], {"event": far}
+            far_out.at[g, ks], x_in.at[g, ks], x_send.at[p + 1], x_recv.at[p + 1],
+            {"event": far},
         ))
         x_copies[-1].start()
     pass_right()
@@ -300,7 +308,12 @@
         ks = pl.ds(first, per)
         near_copies[p].wait_recv()
         base = rad[g, ks, rows(e)] + near_in[g, ks]
-        x_copies[p].wait_recv()
+        if p == 0:
+            x_copies[0].wait_recv()
+            x_copies[1].wait_recv()
+            base = base + cross_in[...]
+        else:
+            x_copies[p + 1].wait_recv()
         nodes[g, ks] = base + x_in[g, ks]
         halo_copies.append(send(
             nodes.at[g, ks], halo_in.at[g, ks], halo_send.at[p], halo_recv.at[g, first // per],
@@ -349,9 +362,15 @@
             table[place, :] = sums[n] if turn == 0 else table[place, :] + sums[n]
 
     pass_left()
-    for number in range(RIM):
-        gram(number)
+    gram(0)
+    gram(1)
     end_left()
+    for p in range(LOADS):
+        arrive(p)
+        if p < 2:
+            gram(2 + p)
+        else:
+            shorten(0, steps, (p - 2) * pairs // 4, (p - 1) * pairs // 4)
     ones = jnp.ones((LANES, LANES), jnp.float32)
 
     def lane_sums(value):
@@ -362,11 +381,9 @@
 
     table[pl.ds(0, 2 * count), :] = jnp.sum(gram_acc[...], axis=1)
     gram_row[...] = lane_sums(table[...])
-    for p in range(LOADS):
-        arrive(p)
-        shorten(0, steps, p * pairs // LOADS, (p + 1) * pairs // LOADS)
     pl.semaphore_wait(ready.at[2], 1)
     gram_copies = spread(gram_row, gram_all, gram_send, gram_recv)
+    shorten(0, steps, pairs // 2, pairs)
     shorten(1, changes, 0, pairs)
     finish(0)
     finish(1)
@@ -460,6 +477,7 @@
     f32, bf16 = jnp.float32, jnp.bfloat16
     vmem, dma = pltpu.VMEM, pltpu.SemaphoreType.DMA
     whole = (2, RIM, part, LANES)
+    per = lons // LOADS
     vmem_spec = pl.BlockSpec(memory_space=pltpu.VMEM)
     any_spec = pl.BlockSpec(memory_space=pl.ANY)
     others = n_c * n_e - 1
@@ -478,6 +496,7 @@
             vmem(whole, f32),
             vmem(whole, f32),
             vmem(whole, f32),
+            vmem((per, part, LANES), f32),
             vmem(whole, f32),
             vmem(whole, f32),
             vmem((all_rows, LANES), f32),
@@ -498,8 +517,8 @@
             dma((LOADS + 2,)),
             dma((2, LOADS)),
             dma((2, LOADS)),
-            dma((LOADS,)),
-            dma((LOADS,)),
+            dma((LOADS + 1,)),
+            dma((LOADS + 1,)),
             dma((LOADS,)),
             dma((2, LOADS // 2)),
             dma((others,)),

time: 23.9 us -> 23.1 us (0.967)
  Pallas kernels: 22.2 us -> 21.4 us
    pallas_call x1, Pallas kernels: 22.2 us -> 21.4 us  [shards(): pl.pallas_call(functools.partial(kernel, (n_c, n_e, pairs, rad_len, lat_l...]
where the time goes in v4:
time: 23.1 us; the launch traced here: 22.9 us
  Pallas kernels  21.4 us (93%)
  local copies, waits for them, and re-layouts  0.82 us (4%)
  between operations  0.64 us (3%)
    pallas_call x1, Pallas kernels, shards(): pl.pallas_call(functools.partial(kernel, (n_c, n_e, pairs, rad_len, lat_l...  21.4 us
    slice x1, local copies, waits for them, and re-layouts, shards(): return (outs[0].reshape(shape), outs[1].reshape(shape))  0.82 us

profile of v4, /device:TPU:0, one launch (start us, length us, event | category | flops | bytes accessed | tf_op | source)
XLA Modules:
  0.0 22.9 jit_solution(13180694402313941038)
XLA Ops:
  0.6 21.4 %shard_map.50 = f32[2,256,256]{2,1,0:T(8,128)S(1)} custom-call(f32[2,4,128,256]{3,2,1,0:T(8,128)} %bitcast.7, f32[8,256,256]{2,1,0:T(8,128)} %bitcast.5, f32[8,256,256]{2,1,0:T(8,128)} %bitcast.6), custom_call_target="tpu_custom_call" | custom-call | tf_op jit(solution)/shard_map/pallas_call | solution.py:485
  22.1 0.8 %fusion = (f32[1,256,256]{2,1,0:T(8,128)}, f32[1,256,256]{2,1,0:T(8,128)}) fusion(f32[2,256,256]{2,1,0:T(8,128)S(1)} %shard_map.50), kind=kLoop, calls=%fused_computation | loop fusion | bytes 1048576 | tf_op jit(solution)/shard_map/slice | solution.py:538

commit v5 on v4

--- a/solution.py
+++ b/solution.py
@@ -9,7 +9,9 @@
 from jax.sharding import PartitionSpec as P
 
 RIM = 4
-LOADS = 4
+UNITS = 4
+CHUNKS = ((0, 0, 2), (0, 2, 2), (1, 0, 2), (1, 2, 2))
+LOADS = len(CHUNKS)
 LANES = 128
 SUB = 8
 MESH = pl.DeviceIdType.MESH
@@ -71,18 +73,6 @@
     def signal(semaphore, **where):
         pl.semaphore_signal(semaphore, 1, device_id=where, device_id_type=MESH)
 
-    for d in range(1, n_e):
-        signal(barrier, event=lax.rem(e + d, n_e))
-    signal(barrier, cuts=flip(1))
-
-    @pl.when(steps_left)
-    def _():
-        signal(barrier, cuts=c - 2)
-
-    @pl.when(steps_right)
-    def _():
-        signal(barrier, cuts=c + 2)
-
     def enter():
         pl.semaphore_wait(barrier, n_e + steps_left.astype(jnp.int32) + steps_right.astype(jnp.int32))
 
@@ -133,15 +123,25 @@
                 others.append({"cuts": where, "event": lax.rem(e + d, n_e)})
 
     sides = (lax.rem(c, 2), 1 - lax.rem(c, 2))
-    per = 2 * RIM // LOADS
-    chunks = [(sides[p * per // RIM], p * per % RIM) for p in range(LOADS)]
+    chunks = [(sides[turn], pl.ds(first, size)) for turn, first, size in CHUNKS]
     loads = []
-    for p, (g, first) in enumerate(chunks):
-        ks = pl.ds(first, per)
+    for p, (g, ks) in enumerate(chunks):
         loads.append(pltpu.make_async_copy(kern_hbm.at[g, ks], kern.at[g, ks], load_sem.at[p]))
         loads[-1].start()
     loads.append(pltpu.make_async_copy(steps_hbm, steps, load_sem.at[LOADS]))
     loads.append(pltpu.make_async_copy(curv_hbm, changes, load_sem.at[LOADS + 1]))
+
+    for d in range(1, n_e):
+        signal(barrier, event=lax.rem(e + d, n_e))
+    signal(barrier, cuts=flip(1))
+
+    @pl.when(steps_left)
+    def _():
+        signal(barrier, cuts=c - 2)
+
+    @pl.when(steps_right)
+    def _():
+        signal(barrier, cuts=c + 2)
 
     matrix = unscaled_gauss(rad_len, 3.0)
     high, low = halves(matrix / jnp.sum(matrix, axis=1, keepdims=True))
@@ -175,8 +175,7 @@
         return out[:, :LANES] + out[:, LANES:]
 
     def exchange(p):
-        g, first = chunks[p]
-        ks = pl.ds(first, per)
+        g, ks = chunks[p]
         if p == 0:
             for number, (where, into) in enumerate(((far, x_in.at[g, ks]), (core_far, cross_in))):
                 x_copies.append(send(
@@ -198,23 +197,23 @@
     for p in range(LOADS + 1):
         before = value
         if p < LOADS:
-            g, first = chunks[p]
+            g, ks = chunks[p]
             loads[p].wait()
             if p == LOADS - 1:
                 for load in loads[LOADS:]:
                     load.start()
             value = packed(
-                kern[g, pl.ds(first, per)].reshape(per * rad_len, lat_len), pack_mat
-            ).reshape(per, rad_len, LANES)
+                kern[g, ks].reshape(ks.size * rad_len, lat_len), pack_mat
+            ).reshape(ks.size, rad_len, LANES)
         if p:
-            high, low = halves(jnp.concatenate([before[k] for k in range(per)], axis=1))
+            g, ks = chunks[p - 1]
+            high, low = halves(jnp.concatenate([before[k] for k in range(ks.size)], axis=1))
             done = jnp.dot(
                 rad_mat[...], jnp.concatenate([high, low, high], axis=0),
                 preferred_element_type=jnp.float32,
             )
-            g, first = chunks[p - 1]
-            for k in range(per):
-                rad[g, first + k] = done[:, k * LANES : (k + 1) * LANES]
+            for k in range(ks.size):
+                rad[g, ks.start + k] = done[:, k * LANES : (k + 1) * LANES]
             if p == 1:
                 enter()
             exchange(p - 1)
@@ -230,8 +229,7 @@
     lat_mat[...] = jnp.concatenate([high, high, low], axis=0)
 
     for copy, p in zip(far_copies, range(1, LOADS)):
-        g, first = chunks[p]
-        ks = pl.ds(first, per)
+        g, ks = chunks[p]
         copy.wait_recv()
         far_out[g, ks] = rad[g, ks, rows(far)] + far_in[g, ks]
         x_copies.append(send(
@@ -247,7 +245,7 @@
     all_rows = steps.shape[1]
     tiles = all_rows // SUB
     lats = lat_len // LANES
-    strip = tiles // RIM
+    strip = tiles // UNITS
 
     def gram(number):
         if number == 0:
@@ -304,8 +302,7 @@
         return row[...] + jnp.sum(slot_refs[...], axis=0)
 
     def arrive(p):
-        g, first = chunks[p]
-        ks = pl.ds(first, per)
+        g, ks = chunks[p]
         near_copies[p].wait_recv()
         base = rad[g, ks, rows(e)] + near_in[g, ks]
         if p == 0:
@@ -316,7 +313,7 @@
             x_copies[p + 1].wait_recv()
         nodes[g, ks] = base + x_in[g, ks]
         halo_copies.append(send(
-            nodes.at[g, ks], halo_in.at[g, ks], halo_send.at[p], halo_recv.at[g, first // per],
+            nodes.at[g, ks], halo_in.at[g, ks], halo_send.at[p], halo_recv.at[p],
             {"cuts": lax.rem(c + n_c - 1 + 2 * g, n_c)},
         ))
         halo_copies[-1].start()
@@ -329,13 +326,13 @@
 
     def finish(turn):
         g = sides[turn]
-        for p in range(turn * LOADS // 2, (turn + 1) * LOADS // 2):
-            first = chunks[p][1]
-            ks = pl.ds(first, per)
-            send(
-                nodes.at[1 - g, ks], halo_in.at[1 - g, ks], halo_send.at[p],
-                halo_recv.at[1 - g, first // per], {"event": core},
-            ).wait_recv()
+        for p, chunk in enumerate(CHUNKS):
+            if chunk[0] == turn:
+                ks = chunks[p][1]
+                send(
+                    nodes.at[1 - g, ks], halo_in.at[1 - g, ks], halo_send.at[p], halo_recv.at[p],
+                    {"event": core},
+                ).wait_recv()
 
         def at(k):
             return k + g * (RIM - 1 - 2 * k)
@@ -362,15 +359,17 @@
             table[place, :] = sums[n] if turn == 0 else table[place, :] + sums[n]
 
     pass_left()
-    gram(0)
-    gram(1)
     end_left()
+    begun = 0
     for p in range(LOADS):
         arrive(p)
-        if p < 2:
-            gram(2 + p)
+        if p < UNITS // 2:
+            gram(p)
         else:
-            shorten(0, steps, (p - 2) * pairs // 4, (p - 1) * pairs // 4)
+            shorten(0, steps, begun, begun + 2)
+            begun += 2
+    for number in range(UNITS // 2, UNITS):
+        gram(number)
     ones = jnp.ones((LANES, LANES), jnp.float32)
 
     def lane_sums(value):
@@ -383,7 +382,7 @@
     gram_row[...] = lane_sums(table[...])
     pl.semaphore_wait(ready.at[2], 1)
     gram_copies = spread(gram_row, gram_all, gram_send, gram_recv)
-    shorten(0, steps, pairs // 2, pairs)
+    shorten(0, steps, begun, pairs)
     shorten(1, changes, 0, pairs)
     finish(0)
     finish(1)
@@ -463,7 +462,7 @@
             direc[place, across] = values[0]
         return 0
 
-    lax.fori_loop(0, tiles, combine, 0, unroll=4)
+    lax.fori_loop(0, tiles, combine, 0, unroll=8)
 
 
 def shards(kernels, steps, curvature):
@@ -477,7 +476,6 @@
     f32, bf16 = jnp.float32, jnp.bfloat16
     vmem, dma = pltpu.VMEM, pltpu.SemaphoreType.DMA
     whole = (2, RIM, part, LANES)
-    per = lons // LOADS
     vmem_spec = pl.BlockSpec(memory_space=pltpu.VMEM)
     any_spec = pl.BlockSpec(memory_space=pl.ANY)
     others = n_c * n_e - 1
@@ -496,7 +494,7 @@
             vmem(whole, f32),
             vmem(whole, f32),
             vmem(whole, f32),
-            vmem((per, part, LANES), f32),
+            vmem((CHUNKS[0][2], part, LANES), f32),
             vmem(whole, f32),
             vmem(whole, f32),
             vmem((all_rows, LANES), f32),
@@ -520,7 +518,7 @@
             dma((LOADS + 1,)),
             dma((LOADS + 1,)),
             dma((LOADS,)),
-            dma((2, LOADS // 2)),
+            dma((LOADS,)),
             dma((others,)),
             dma((others,)),
             dma((others,)),

time: 23.1 us -> 22.3 us (0.965)
  Pallas kernels: 21.4 us -> 20.7 us
    pallas_call x1, Pallas kernels: 21.4 us -> 20.7 us  [shards(): pl.pallas_call(functools.partial(kernel, (n_c, n_e, pairs, rad_len, lat_l...]
where the time goes in v5:
time: 22.3 us; the launch traced here: 22.2 us
  Pallas kernels  20.7 us (93%)
  local copies, waits for them, and re-layouts  0.82 us (4%)
  between operations  0.64 us (3%)
    pallas_call x1, Pallas kernels, shards(): pl.pallas_call(functools.partial(kernel, (n_c, n_e, pairs, rad_len, lat_l...  20.7 us
    slice x1, local copies, waits for them, and re-layouts, shards(): return (outs[0].reshape(shape), outs[1].reshape(shape))  0.82 us

profile of v5, /device:TPU:0, one launch (start us, length us, event | category | flops | bytes accessed | tf_op | source)
XLA Modules:
  0.0 22.2 jit_solution(4253907605788306249)
XLA Ops:
  0.6 20.7 %shard_map.50 = f32[2,256,256]{2,1,0:T(8,128)S(1)} custom-call(f32[2,4,128,256]{3,2,1,0:T(8,128)} %bitcast.7, f32[8,256,256]{2,1,0:T(8,128)} %bitcast.5, f32[8,256,256]{2,1,0:T(8,128)} %bitcast.6), custom_call_target="tpu_custom_call" | custom-call | tf_op jit(solution)/shard_map/pallas_call | solution.py:483
  21.4 0.8 %fusion = (f32[1,256,256]{2,1,0:T(8,128)}, f32[1,256,256]{2,1,0:T(8,128)}) fusion(f32[2,256,256]{2,1,0:T(8,128)S(1)} %shard_map.50), kind=kLoop, calls=%fused_computation | loop fusion | bytes 1048576 | tf_op jit(solution)/shard_map/slice | solution.py:536

commit v6 on v5

--- a/solution.py
+++ b/solution.py
@@ -288,17 +288,13 @@
                     else:
                         gram_acc[place] = gram_acc[place] + sums[2 * m + kind]
 
-    def spread(row, slot_refs, sends, recvs):
+    def spread(row, slot_refs, sent, landed):
         for d, other in enumerate(others):
-            send(row, slot_refs.at[d], sends.at[d], recvs.at[d], other).start()
-        return [
-            send(row, slot_refs.at[d], sends.at[d], recvs.at[d], other)
-            for d, other in enumerate(others)
-        ]
-
-    def gathered(row, slot_refs, copies):
-        for copy in copies:
-            copy.wait_recv()
+            send(row, slot_refs.at[d], sent, landed, other).start()
+        return send(slot_refs, slot_refs, sent, landed, others[0])
+
+    def gathered(row, slot_refs, copy):
+        copy.wait_recv()
         return row[...] + jnp.sum(slot_refs[...], axis=0)
 
     def arrive(p):
@@ -381,7 +377,7 @@
     table[pl.ds(0, 2 * count), :] = jnp.sum(gram_acc[...], axis=1)
     gram_row[...] = lane_sums(table[...])
     pl.semaphore_wait(ready.at[2], 1)
-    gram_copies = spread(gram_row, gram_all, gram_send, gram_recv)
+    gram_copies = spread(gram_row, gram_all, gram_send.at[0], gram_recv.at[0])
     shorten(0, steps, begun, pairs)
     shorten(1, changes, 0, pairs)
     finish(0)
@@ -392,7 +388,7 @@
         jnp.ones((SUB, 3 * LANES), jnp.bfloat16), jnp.concatenate([first, second, third], axis=1),
         (((1,), (1,)), ((), ())), preferred_element_type=jnp.float32,
     )[:1]
-    late_copies = spread(late_row, late_all, late_send, late_recv)
+    late_copies = spread(late_row, late_all, late_send.at[0], late_recv.at[0])
     high, low = halves(smooth[...])
     grad[...] = jnp.dot(
         jnp.concatenate([high, low, high], axis=1), lat_mat[...],
@@ -438,7 +434,7 @@
         mix[i : i + 1, :] = -onto[i]
         mix[pairs + i : pairs + i + 1, :] = scaling * alphas[i]
 
-    for copies in (far_copies, near_copies, x_copies, halo_copies, gram_copies, late_copies):
+    for copies in (far_copies, near_copies, x_copies, halo_copies, (gram_copies, late_copies)):
         for copy in copies:
             copy.wait_send()
     products = gathered(late_row, late_all, late_copies)
@@ -519,10 +515,10 @@
             dma((LOADS + 1,)),
             dma((LOADS,)),
             dma((LOADS,)),
-            dma((others,)),
-            dma((others,)),
-            dma((others,)),
-            dma((others,)),
+            dma((1,)),
+            dma((1,)),
+            dma((1,)),
+            dma((1,)),
         ],
         compiler_params=pltpu.CompilerParams(
             collective_id=0, has_side_effects=True, vmem_limit_bytes=61905306

time: 22.3 us -> 21.2 us (0.951)
  Pallas kernels: 20.7 us -> 19.6 us
    pallas_call x1, Pallas kernels: 20.7 us -> 19.6 us  [shards(): pl.pallas_call(functools.partial(kernel, (n_c, n_e, pairs, rad_len, lat_l...]
where the time goes in v6:
time: 21.2 us; the launch traced here: 21.1 us
  Pallas kernels  19.6 us (92%)
  local copies, waits for them, and re-layouts  0.82 us (4%)
  between operations  0.64 us (3%)
    pallas_call x1, Pallas kernels, shards(): pl.pallas_call(functools.partial(kernel, (n_c, n_e, pairs, rad_len, lat_l...  19.6 us
    slice x1, local copies, waits for them, and re-layouts, shards(): return (outs[0].reshape(shape), outs[1].reshape(shape))  0.82 us

profile of v6, /device:TPU:0, one launch (start us, length us, event | category | flops | bytes accessed | tf_op | source)
XLA Modules:
  0.0 21.1 jit_solution(4517991314548023981)
XLA Ops:
  0.6 19.6 %shard_map.50 = f32[2,256,256]{2,1,0:T(8,128)S(1)} custom-call(f32[2,4,128,256]{3,2,1,0:T(8,128)} %bitcast.7, f32[8,256,256]{2,1,0:T(8,128)} %bitcast.5, f32[8,256,256]{2,1,0:T(8,128)} %bitcast.6), custom_call_target="tpu_custom_call" | custom-call | tf_op jit(solution)/shard_map/pallas_call | solution.py:479
  20.2 0.8 %fusion = (f32[1,256,256]{2,1,0:T(8,128)}, f32[1,256,256]{2,1,0:T(8,128)}) fusion(f32[2,256,256]{2,1,0:T(8,128)S(1)} %shard_map.50), kind=kLoop, calls=%fused_computation | loop fusion | bytes 1048576 | tf_op jit(solution)/shard_map/slice | solution.py:532

commit v7 on v6

--- a/solution.py
+++ b/solution.py
@@ -189,7 +189,7 @@
             if p or number:
                 copies.append(send(
                     rad.at[g, ks, rows(chunk)], into.at[g, ks],
-                    core_send.at[number, p], core_recv.at[number, p], {"event": core},
+                    core_send.at[0 if number else p], core_recv.at[0 if number else p], {"event": core},
                 ))
                 copies[-1].start()
 
@@ -297,9 +297,12 @@
         copy.wait_recv()
         return row[...] + jnp.sum(slot_refs[...], axis=0)
 
+    near_all = send(near_in, near_in, core_send.at[0], core_recv.at[0], {"event": core})
+
     def arrive(p):
         g, ks = chunks[p]
-        near_copies[p].wait_recv()
+        if p == 0:
+            near_all.wait_recv()
         base = rad[g, ks, rows(e)] + near_in[g, ks]
         if p == 0:
             x_copies[0].wait_recv()
@@ -309,26 +312,28 @@
             x_copies[p + 1].wait_recv()
         nodes[g, ks] = base + x_in[g, ks]
         halo_copies.append(send(
-            nodes.at[g, ks], halo_in.at[g, ks], halo_send.at[p], halo_recv.at[p],
+            nodes.at[g, ks], halo_in.at[g, ks], halo_send.at[CHUNKS[p][0]], halo_recv.at[CHUNKS[p][0]],
             {"cuts": lax.rem(c + n_c - 1 + 2 * g, n_c)},
         ))
         halo_copies[-1].start()
 
     def shorten(kind, vector, first, last):
-        for i in range(first, last):
-            short[kind * pairs + i] = packed(vector[i], dual_mat)
+        for i in range(first, last, 2):
+            place = pl.ds(kind * pairs + i, 2)
+            short[place] = packed(
+                vector[pl.ds(i, 2)].reshape(2 * all_rows, lat_len), dual_mat
+            ).reshape(2, all_rows, LANES)
 
     weights = cycle_weights()
 
     def finish(turn):
         g = sides[turn]
-        for p, chunk in enumerate(CHUNKS):
-            if chunk[0] == turn:
-                ks = chunks[p][1]
-                send(
-                    nodes.at[1 - g, ks], halo_in.at[1 - g, ks], halo_send.at[p], halo_recv.at[p],
-                    {"event": core},
-                ).wait_recv()
+        halo_all = send(
+            halo_in.at[1 - g], halo_in.at[1 - g], halo_send.at[turn], halo_recv.at[turn],
+            {"event": core},
+        )
+        halo_all.wait_recv()
+        halo_all.wait_send()
 
         def at(k):
             return k + g * (RIM - 1 - 2 * k)
@@ -359,12 +364,12 @@
     begun = 0
     for p in range(LOADS):
         arrive(p)
-        if p < UNITS // 2:
+        if p < 3:
             gram(p)
         else:
             shorten(0, steps, begun, begun + 2)
             begun += 2
-    for number in range(UNITS // 2, UNITS):
+    for number in range(3, UNITS):
         gram(number)
     ones = jnp.ones((LANES, LANES), jnp.float32)
 
@@ -434,7 +439,7 @@
         mix[i : i + 1, :] = -onto[i]
         mix[pairs + i : pairs + i + 1, :] = scaling * alphas[i]
 
-    for copies in (far_copies, near_copies, x_copies, halo_copies, (gram_copies, late_copies)):
+    for copies in (far_copies, x_copies, (near_all, gram_copies, late_copies)):
         for copy in copies:
             copy.wait_send()
     products = gathered(late_row, late_all, late_copies)
@@ -509,12 +514,12 @@
             vmem((others, 1, LANES), f32),
             pltpu.SemaphoreType.REGULAR((3,)),
             dma((LOADS + 2,)),
-            dma((2, LOADS)),
-            dma((2, LOADS)),
+            dma((LOADS,)),
+            dma((LOADS,)),
             dma((LOADS + 1,)),
             dma((LOADS + 1,)),
-            dma((LOADS,)),
-            dma((LOADS,)),
+            dma((2,)),
+            dma((2,)),
             dma((1,)),
             dma((1,)),
             dma((1,)),

time: 21.2 us -> 21.1 us (level)
  no operation moved by 1% of the time
where the time goes in v7:
time: 21.1 us; the launch traced here: 21 us
  Pallas kernels  19.5 us (92%)
  local copies, waits for them, and re-layouts  0.82 us (4%)
  between operations  0.64 us (3%)
    pallas_call x1, Pallas kernels, shards(): pl.pallas_call(functools.partial(kernel, (n_c, n_e, pairs, rad_len, lat_l...  19.5 us
    slice x1, local copies, waits for them, and re-layouts, shards(): return (outs[0].reshape(shape), outs[1].reshape(shape))  0.82 us

profile of v7, /device:TPU:0, one launch (start us, length us, event | category | flops | bytes accessed | tf_op | source)
XLA Modules:
  0.0 21.0 jit_solution(2735013024057177635)
XLA Ops:
  0.6 19.5 %shard_map.50 = f32[2,256,256]{2,1,0:T(8,128)S(1)} custom-call(f32[2,4,128,256]{3,2,1,0:T(8,128)} %bitcast.7, f32[8,256,256]{2,1,0:T(8,128)} %bitcast.5, f32[8,256,256]{2,1,0:T(8,128)} %bitcast.6), custom_call_target="tpu_custom_call" | custom-call | tf_op jit(solution)/shard_map/pallas_call | solution.py:484
  20.2 0.8 %fusion = (f32[1,256,256]{2,1,0:T(8,128)}, f32[1,256,256]{2,1,0:T(8,128)}) fusion(f32[2,256,256]{2,1,0:T(8,128)S(1)} %shard_map.50), kind=kLoop, calls=%fused_computation | loop fusion | bytes 1048576 | tf_op jit(solution)/shard_map/slice | solution.py:537
